TPU v7x, 256 devices: a 4x2x16 block of a 4x16x16 slice. The times are simulated.
256 devices in a mesh: groups: 2 (over y), grid: 32 (over z, core), depth: 4 (over x).
Axes of the slice: x: 4, y: 2, z: 16, core: 2. Of those that a mesh axis runs over, the one named last changes fastest.
The devices are a block of a 4x16x16 slice.
Arguments:
- tokens: bfloat16 [4096, 4096], P(('groups', 'grid'), 'depth'), parts along dimension 0, may hold values from -6 to 6
- gate_weight: bfloat16 [4096, 14336], P('depth', 'grid'), may hold values from -0.09375 to 0.09375
- up_weight: bfloat16 [4096, 14336], P('depth', 'grid'), may hold values from -0.09375 to 0.09375
- down_weight: bfloat16 [14336, 4096], P('grid', 'depth'), may hold values from -0.046875 to 0.046875
Outputs:
- mixed: bfloat16 [4096, 4096], P(('groups', 'grid'), 'depth'), parts along dimension 0
There are 2 independent parts, one for each index of `groups`. A program takes and returns all parts, laid end to end along the dimension named above; an argument that names none is the same for every part. Nothing has to cross between parts.
All inputs are finite; a program needn't handle non-finite values.
Results may differ from a plain program's by a relative error of at most 0.0049.
Values may be sent and summed in bfloat16 or wider, within the bound.
A program may use at most 64 MiB of HBM per device.

v0:
```python
import jax
import jax.numpy as jnp
from jax import lax
from jax.sharding import Mesh
from jax.sharding import PartitionSpec as P

GRID = ("grid_0", "grid_1")
GROUPS_GRID = ("groups", "grid_0", "grid_1")


def joined_along(blocks, dim):
    shape = list(blocks.shape[1:])
    shape[dim] *= blocks.shape[0]
    return jnp.moveaxis(blocks, 0, dim).reshape(shape)


def sent_to_all(value, axis):
    copies = jnp.broadcast_to(value, (lax.axis_size(axis), *value.shape))
    return lax.all_to_all(copies, axis, split_axis=0, concat_axis=0, tiled=True)


def gathered_copies(value, axis, dim):
    return joined_along(sent_to_all(value, axis), dim)


def own_block(blocks, axes, sequence):
    shape = [lax.axis_size(a) for a in axes]
    blocks = blocks.reshape(*shape, *blocks.shape[1:])
    blocks = blocks.transpose(*sequence, *range(len(axes), blocks.ndim))
    blocks = blocks.reshape(-1, *blocks.shape[len(axes) :])
    for k in sequence:
        blocks = lax.psum_scatter(blocks, axes[k], scatter_dimension=0, tiled=True)
    return blocks[0]


def cut_along(value, dim, length):
    shape = value.shape
    blocks = value.reshape(*shape[:dim], length, shape[dim] // length, *shape[dim + 1 :])
    return jnp.moveaxis(blocks, dim, 0)


def scatter_axes(value, axes, sequence, dim):
    length = lax.axis_size(axes)
    return own_block(cut_along(value, dim, length), axes, sequence)


def body(tokens, gate_weight, up_weight, down_weight):
    grid_size = lax.axis_size(GRID)
    block_rows = tokens.shape[0]
    total_rows = block_rows * grid_size
    width_share = gate_weight.shape[1]
    stacked = jnp.concatenate([gate_weight, up_weight], axis=1)
    pre_act = jnp.dot(
        lax.all_gather(tokens, GRID, axis=0, tiled=True),
        stacked,
        preferred_element_type=jnp.float32,
    )
    blocked = pre_act.reshape(grid_size, block_rows, 2 * width_share)
    summed = lax.psum_scatter(blocked, "depth", scatter_dimension=1, tiled=True)
    hidden = gathered_copies(
        (jax.nn.silu(summed[..., :width_share]) * summed[..., width_share:]).astype(jnp.bfloat16),
        "depth",
        1,
    ).reshape(total_rows, width_share)
    return scatter_axes(
        jnp.dot(hidden, down_weight, preferred_element_type=jnp.float32), GRID, (1, 0), 0
    ).astype(jnp.bfloat16)


def solution(mesh):
    torus = Mesh(
        mesh.devices.reshape(mesh.shape["groups"], 16, 2, mesh.shape["depth"]),
        ("groups", "grid_0", "grid_1", "depth"),
    )
    placed = (P(GROUPS_GRID, "depth"), P("depth", GRID), P("depth", GRID), P(GRID, "depth"))
    return jax.shard_map(
        body, mesh=torus, in_specs=placed, out_specs=P(GROUPS_GRID, "depth"), check_vma=False
    )
```

profile of v0, /device:TPU:34, one launch (start us, length us, event | category | flops | bytes accessed | tf_op | source)
XLA Modules:
  0.0 342.8 jit_solution(1183751066836995780)
XLA Ops:
  6.5 0.0 copy-start
  6.6 0.0 all-gather.2.cloned.1.call-start
  6.6 0.7 all-gather.2.cloned.1.call-update
  7.3 0.1 reduce-scatter.4.cloned.1.call-start
  7.4 87.2 %all-gather.2.cloned.1.call-done = bf16[2048,1024]{1,0:T(8,128)(2,1)} async-done(((bf16[64,1024]{1,0:T(8,128)(2,1)}), bf16[2048,1024]{1,0:T(8,128)(2,1)}) %all-gather.2.cloned.1.call-update) | async-done | bytes 4194320 | tf_op jit(solution)/shard_map/all_gather | solution.py:54
  94.6 9.7 %convolution_bitcast_fusion = f32[2048,896]{0,1:T(8,128)} fusion(bf16[2048,1024]{1,0:T(8,128)(2,1)} %all-gather.2.cloned.1.call-done, bf16[1024,448]{0,1:T(8,128)(2,1)} %param.6, bf16[1024,448]{0,1:T(8,128)(2,1)} %param.5), kind=kOutput, calls=%fused_computation | convolution fusion | flops 3761766400 | bytes 13369344 | tf_op jit(solution)/shard_map/dot_general | solution.py:53
  104.3 8.6 %copy.8 = f32[2048,896]{1,0:T(8,128)} copy(f32[2048,896]{0,1:T(8,128)} %convolution_bitcast_fusion) | data formatting | bytes 14680064 | tf_op jit(solution)/shard_map/dot_general | solution.py:53
  112.9 0.1 reduce-scatter.4.cloned.1.call-update
  112.9 0.1 reduce-scatter.6.cloned.1.call-start
  113.0 74.8 %reduce-scatter.4.cloned.1.call-done = f32[32,16,896]{2,1,0:T(8,128)} async-done(((f32[32,64,896]{2,1,0:T(8,128)}), f32[32,16,896]{2,1,0:T(8,128)}) %reduce-scatter.4.cloned.1.call-update) | async-done | bytes 1835024 | tf_op jit(solution)/shard_map/reduce_scatter | solution.py:59
  187.7 1.9 fusion.3
  189.7 0.3 broadcast_in_dim.3
  190.0 29.4 %all_to_all.5 = bf16[4,32,16,448]{3,2,1,0:T(8,128)(2,1)S(1)} all-to-all(bf16[4,32,16,448]{3,2,1,0:T(8,128)(2,1)S(1)} %broadcast_in_dim.3), channel_id=1, replica_groups=mesh['groups'=2,'grid_0'=16,'grid_1'=2,'depth'=4] {'depth'}, dimensions={0} | all-to-all | bytes 3670016 | tf_op jit(solution)/shard_map/all_to_all | solution.py:19
  219.4 0.2 copy.9
  219.6 0.0 copy-done
  219.6 2.4 convolution_bitcast_fusion.1
  222.0 4.1 %copy.10 = f32[2,16,64,1024]{3,2,1,0:T(8,128)} copy(f32[2,16,64,1024]{3,2,0,1:T(8,128)S(1)} %convolution_bitcast_fusion.1) | data formatting | bytes 16777216 | tf_op jit(solution)/shard_map/transpose | solution.py:29
  226.0 0.1 reduce-scatter.6.cloned.1.call-update
  226.1 0.1 reduce-scatter.8.cloned.1.call-start
  226.2 25.8 %reduce-scatter.6.cloned.1.call-done = f32[16,64,1024]{2,1,0:T(8,128)} async-done(((f32[32,64,1024]{2,1,0:T(8,128)}), f32[16,64,1024]{2,1,0:T(8,128)}) %reduce-scatter.6.cloned.1.call-update) | async-done | bytes 4194320 | tf_op jit(solution)/shard_map/reduce_scatter | solution.py:32
  252.0 0.1 reduce-scatter.8.cloned.1.call-update
  252.0 82.6 %reduce-scatter.8.cloned.1.call-done = f32[1,64,1024]{2,1,0:T(8,128)} async-done(((f32[16,64,1024]{2,1,0:T(8,128)}), f32[1,64,1024]{2,1,0:T(8,128)}) %reduce-scatter.8.cloned.1.call-update) | async-done | bytes 262160 | tf_op jit(solution)/shard_map/reduce_scatter | solution.py:32
  334.6 1.6 convert_bitcast_fusion
Async XLA Ops:
  6.5 213.1 %copy-start = (bf16[448,1024]{1,0:T(8,128)(2,1)S(1)}, bf16[448,1024]{1,0:T(8,128)(2,1)}, u32[]{:S(2)}) copy-start(bf16[448,1024]{1,0:T(8,128)(2,1)} %param.7) | copy-start | bytes 2752516
  6.6 88.0 %all-gather.2.cloned.1.call-start = ((), (), s32[]{:S(2)}) async-start(), calls=%async_computation.4 | async-start | bytes 4325376 | tf_op jit(solution)/shard_map/all_gather | solution.py:54
  7.3 180.4 %reduce-scatter.4.cloned.1.call-start = ((), (), s32[]{:S(2)}) async-start(), calls=%async_computation.5 | async-start | bytes 9175040 | tf_op jit(solution)/shard_map/reduce_scatter | solution.py:59
  112.9 139.1 %reduce-scatter.6.cloned.1.call-start = ((), (), s32[]{:S(2)}) async-start(), calls=%async_computation.6 | async-start | bytes 12582912 | tf_op jit(solution)/shard_map/reduce_scatter | solution.py:32
  226.1 108.5 %reduce-scatter.8.cloned.1.call-start = ((), (), s32[]{:S(2)}) async-start(), calls=%async_computation.7 | async-start | bytes 4456448 | tf_op jit(solution)/shard_map/reduce_scatter | solution.py:32
Sparse Core Ops, SparseCore 0:
  9.2 85.3 all-gather.1
  113.0 74.6 reduce-scatter.3
  226.2 25.7 reduce-scatter.5
  254.4 80.1 reduce-scatter.7
where the time goes:
time: 343 us
  waiting for transfers between devices  271 us (79%)
  blocking collectives  29.4 us (9%)
  between operations  13.2 us (4%)
  local copies, waits for them, and re-layouts  13.1 us (4%)
  matrix products  12.1 us (4%)
  other arithmetic  3.57 us (1%)
    reduce_scatter x2, waiting for transfers between devices, own_block(): blocks = lax.psum_scatter(blocks, axes[k], scatter_dimension=0, tiled=True)  108 us
    all_gather x1, waiting for transfers between devices, body(): lax.all_gather(tokens, GRID, axis=0, tiled=True)  87.2 us
    reduce_scatter x1, waiting for transfers between devices, body(): summed = lax.psum_scatter(blocked, 'depth', scatter_dimension=1, tiled=True)  74.8 us
    all_to_all x1, blocking collectives, sent_to_all(): return lax.all_to_all(copies, axis, split_axis=0, concat_axis=0, tiled=True)  29.4 us
    dot_general x1, matrix products, body(): jnp.dot(lax.all_gather(tokens, GRID, axis=0, tiled=True), stacked, prefer...  9.7 us
    dot_general x1, local copies, waits for them, and re-layouts, body(): jnp.dot(lax.all_gather(tokens, GRID, axis=0, tiled=True), stacked, prefer...  8.59 us
  transfers between devices with their start and end apart: 4, of which 4 were waited for; matrix products, arithmetic and copies ran while one was open for 0% of the time, Pallas kernels for 0%

commit v1 on v0

--- a/solution.py
+++ b/solution.py
@@ -3,6 +3,7 @@
 from jax import lax
 from jax.sharding import Mesh
 from jax.sharding import PartitionSpec as P
+from jax.lax import all_to_all, axis_size
 
 GRID = ("grid_0", "grid_1")
 GROUPS_GRID = ("groups", "grid_0", "grid_1")
@@ -51,7 +52,15 @@
     width_share = gate_weight.shape[1]
     stacked = jnp.concatenate([gate_weight, up_weight], axis=1)
     pre_act = jnp.dot(
-        lax.all_gather(tokens, GRID, axis=0, tiled=True),
+        jnp.concatenate(
+            all_to_all(
+                jnp.stack([tokens for _ in range(axis_size(GRID))]),
+                axis_name=GRID,
+                split_axis=0,
+                concat_axis=0,
+            ),
+            0,
+        ),
         stacked,
         preferred_element_type=jnp.float32,
     )

time: 343 us -> 463 us (1.35)
  blocking collectives: 29.4 us -> 244 us
  waiting for transfers between devices: 271 us -> 179 us
    all_to_all x0 -> x1, blocking collectives: none -> 215 us  [body(): all_to_all(jnp.stack([tokens for _ in range(axis_size(GRID))]), axis_name...]
    all_gather x1 -> x0, waiting for transfers between devices: 87.2 us -> none  [body(): lax.all_gather(tokens, GRID, axis=0, tiled=True)]
    reduce_scatter x1, waiting for transfers between devices: 74.8 us -> 70 us  [body(): summed = lax.psum_scatter(blocked, 'depth', scatter_dimension=1, tiled=True)]
  transfers between devices with their start and end apart: 4 -> 3, of which waited for: 4 -> 3; matrix products, arithmetic and copies ran while one was open for 0% -> 0% of each run, Pallas kernels for 0% -> 0%
where the time goes in v1:
time: 463 us
  blocking collectives  244 us (53%)
  waiting for transfers between devices  179 us (39%)
  local copies, waits for them, and re-layouts  14.7 us (3%)
  between operations  13.2 us (3%)
  matrix products  8.37 us (2%)
    all_to_all x1, blocking collectives, body(): all_to_all(jnp.stack([tokens for _ in range(axis_size(GRID))]), axis_name...  215 us
    reduce_scatter x2, waiting for transfers between devices, own_block(): blocks = lax.psum_scatter(blocks, axes[k], scatter_dimension=0, tiled=True)  109 us
    reduce_scatter x1, waiting for transfers between devices, body(): summed = lax.psum_scatter(blocked, 'depth', scatter_dimension=1, tiled=True)  70 us
    all_to_all x1, blocking collectives, sent_to_all(): return lax.all_to_all(copies, axis, split_axis=0, concat_axis=0, tiled=True)  29.4 us
  transfers between devices with their start and end apart: 3, of which 3 were waited for; matrix products, arithmetic and copies ran while one was open for 0% of the time, Pallas kernels for 0%

profile of v1, /device:TPU:34, one launch (start us, length us, event | category | flops | bytes accessed | tf_op | source)
XLA Modules:
  0.0 462.8 jit_solution(16266222521219105657)
XLA Ops:
  6.5 0.0 copy-start
  6.6 0.0 reduce-scatter.4.cloned.1.call-start
  6.6 1.5 stack.2
  8.1 0.0 copy-start.1
  8.1 0.0 copy-start.2
  8.1 214.8 %all_to_all.10 = bf16[32,64,1024]{2,1,0:T(8,128)(2,1)S(1)} all-to-all(bf16[32,64,1024]{2,1,0:T(8,128)(2,1)S(1)} %stack.2), channel_id=1, replica_groups=mesh['groups'=2,'grid_0'=16,'grid_1'=2,'depth'=4] {'grid_0','grid_1'}, dimensions={0} | all-to-all | bytes 8388608 | tf_op jit(solution)/shard_map/all_to_all | solution.py:56
  222.9 0.0 copy-done.1
  222.9 0.0 copy-done.2
  222.9 6.0 %convolution_bitcast_fusion = f32[2048,896]{0,1:T(8,128)} fusion(bf16[2048,1024]{1,0:T(8,128)(2,1)S(1)} %bitcast.21, bf16[1024,448]{0,1:T(8,128)(2,1)S(1)} %copy-done.1, bf16[1024,448]{0,1:T(8,128)(2,1)S(1)} %copy-done.2), kind=kOutput, calls=%fused_computation | convolution fusion | flops 3761766400 | bytes 13369344 | tf_op jit(solution)/shard_map/dot_general | solution.py:54
  228.9 8.6 %copy.8 = f32[2048,896]{1,0:T(8,128)} copy(f32[2048,896]{0,1:T(8,128)} %convolution_bitcast_fusion) | data formatting | bytes 14680064 | tf_op jit(solution)/shard_map/dot_general | solution.py:54
  237.5 0.1 reduce-scatter.4.cloned.1.call-update
  237.6 0.1 reduce-scatter.6.cloned.1.call-start
  237.6 70.0 %reduce-scatter.4.cloned.1.call-done = f32[32,16,896]{2,1,0:T(8,128)} async-done(((f32[32,64,896]{2,1,0:T(8,128)}), f32[32,16,896]{2,1,0:T(8,128)}) %reduce-scatter.4.cloned.1.call-update) | async-done | bytes 1835024 | tf_op jit(solution)/shard_map/reduce_scatter | solution.py:68
  307.7 1.9 fusion.3
  309.6 0.3 broadcast_in_dim.3
  309.9 29.4 %all_to_all.11 = bf16[4,32,16,448]{3,2,1,0:T(8,128)(2,1)S(1)} all-to-all(bf16[4,32,16,448]{3,2,1,0:T(8,128)(2,1)S(1)} %broadcast_in_dim.3), channel_id=1, replica_groups=mesh['groups'=2,'grid_0'=16,'grid_1'=2,'depth'=4] {'depth'}, dimensions={0} | all-to-all | bytes 3670016 | tf_op jit(solution)/shard_map/all_to_all | solution.py:20
  339.3 0.2 copy.9
  339.5 0.0 copy-done
  339.5 2.3 convolution_bitcast_fusion.1
  341.9 4.1 copy.10
  346.0 0.1 reduce-scatter.6.cloned.1.call-update
  346.0 0.1 reduce-scatter.8.cloned.1.call-start
  346.1 25.8 %reduce-scatter.6.cloned.1.call-done = f32[16,64,1024]{2,1,0:T(8,128)} async-done(((f32[32,64,1024]{2,1,0:T(8,128)}), f32[16,64,1024]{2,1,0:T(8,128)}) %reduce-scatter.6.cloned.1.call-update) | async-done | bytes 4194320 | tf_op jit(solution)/shard_map/reduce_scatter | solution.py:33
  371.9 0.1 reduce-scatter.8.cloned.1.call-update
  371.9 82.7 %reduce-scatter.8.cloned.1.call-done = f32[1,64,1024]{2,1,0:T(8,128)} async-done(((f32[16,64,1024]{2,1,0:T(8,128)}), f32[1,64,1024]{2,1,0:T(8,128)}) %reduce-scatter.8.cloned.1.call-update) | async-done | bytes 262160 | tf_op jit(solution)/shard_map/reduce_scatter | solution.py:33
  454.7 1.6 convert_bitcast_fusion
Async XLA Ops:
  6.5 333.0 %copy-start = (bf16[448,1024]{1,0:T(8,128)(2,1)S(1)}, bf16[448,1024]{1,0:T(8,128)(2,1)}, u32[]{:S(2)}) copy-start(bf16[448,1024]{1,0:T(8,128)(2,1)} %param.7) | copy-start | bytes 2752516
  6.6 301.1 %reduce-scatter.4.cloned.1.call-start = ((), (), s32[]{:S(2)}) async-start(), calls=%async_computation.5 | async-start | bytes 9175040 | tf_op jit(solution)/shard_map/reduce_scatter | solution.py:68
  8.1 214.8 %copy-start.1 = (bf16[1024,448]{0,1:T(8,128)(2,1)S(1)}, bf16[1024,448]{0,1:T(8,128)(2,1)}, u32[]{:S(2)}) copy-start(bf16[1024,448]{0,1:T(8,128)(2,1)} %param.6) | copy-start | bytes 2752516
  8.1 214.8 %copy-start.2 = (bf16[1024,448]{0,1:T(8,128)(2,1)S(1)}, bf16[1024,448]{0,1:T(8,128)(2,1)}, u32[]{:S(2)}) copy-start(bf16[1024,448]{0,1:T(8,128)(2,1)} %param.5) | copy-start | bytes 2752516
  237.6 134.3 %reduce-scatter.6.cloned.1.call-start = ((), (), s32[]{:S(2)}) async-start(), calls=%async_computation.6 | async-start | bytes 12582912 | tf_op jit(solution)/shard_map/reduce_scatter | solution.py:33
  346.0 108.7 %reduce-scatter.8.cloned.1.call-start = ((), (), s32[]{:S(2)}) async-start(), calls=%async_computation.7 | async-start | bytes 4456448 | tf_op jit(solution)/shard_map/reduce_scatter | solution.py:33
Sparse Core Ops, SparseCore 0:
  237.7 69.9 reduce-scatter.3
  346.1 25.6 reduce-scatter.5
  374.5 80.1 reduce-scatter.7
